TPU v7x, 32 devices: a whole 2x2x4 slice. The times are simulated.
32 devices in a mesh: cfg: 2 (over y), expert: 4 (over z), ffn: 4 (over x, core).
Axes of the slice: x: 2, y: 2, z: 4, core: 2. Of those that a mesh axis runs over, the one named last changes fastest.
Arguments:
- tokens: bfloat16 [2048, 2048], P(('cfg', 'expert'), 'ffn'), parts along dimension 0, may hold values from -6 to 6
- chosen: int32 [8, 512], P(('cfg', 'expert')), parts along dimension 0, may hold values from 0 to 1023, as said below
- gates: float32 [8, 512], P(('cfg', 'expert')), parts along dimension 0, may hold values from 0.1 to 1
- capacity: int32 [2], P('cfg'), parts along dimension 0, may hold values from 256 to 512
- w_gate: bfloat16 [4, 2048, 1024], P('expert', None, 'ffn'), may hold values from -0.125 to 0.125
- w_up: bfloat16 [4, 2048, 1024], P('expert', None, 'ffn'), may hold values from -0.125 to 0.125
- w_down: bfloat16 [4, 1024, 2048], P('expert', 'ffn'), may hold values from -0.1875 to 0.1875
Outputs:
- mixed: bfloat16 [2048, 2048], P(('cfg', 'expert'), 'ffn'), parts along dimension 0
There are 2 independent parts, one for each index of `cfg`. A program takes and returns all parts, laid end to end along the dimension named above; an argument that names none is the same for every part. Nothing has to cross between parts.
Inputs may be any that keep to these rules, and one draw needn't show every extreme that they name: `chosen`: each row lists 512 different tokens; at most 256 of one row's tokens lie in one aligned block of 256 tokens, and every row has exactly 256 in some block.
All inputs are finite; a program needn't handle non-finite values.
Results may differ from a plain program's by a relative error of at most 0.013.
Values may be sent and summed in bfloat16 or wider, within the bound.
A program may use at most 64 MiB of HBM per device.

v0:
```python
import functools

import jax
import jax.numpy as jnp
from jax import lax
from jax.experimental import pallas as pl
from jax.experimental.pallas import tpu as pltpu
from jax.sharding import PartitionSpec as P


def shards_general(tokens, chosen, gates, capacity, w_gate, w_up, w_down):
    experts_n = lax.axis_size("expert")
    tok_dev = tokens.shape[0]
    picked_ids = chosen[0]
    listed = picked_ids.shape[0]
    slot_depth = 2 * listed // experts_n
    positions = jnp.arange(listed, dtype=jnp.int32)
    alive_mask = positions < capacity[0]
    weights = jnp.where(alive_mask, gates[0], jnp.zeros_like(gates[0]))
    source = picked_ids // tok_dev
    offset = picked_ids - source * tok_dev
    member = (source[:, None] == jnp.arange(experts_n, dtype=jnp.int32)[None, :]).astype(jnp.int32)
    before = jnp.cumsum(member, axis=0) - member
    rank_in = jnp.sum(before * member, axis=1)
    slot_of = source * slot_depth + rank_in
    wanted = jnp.where(alive_mask, offset, -1)
    request = jnp.full((experts_n * slot_depth,), -1, jnp.int32).at[slot_of].set(wanted)
    requested = lax.all_to_all(
        request.reshape(experts_n, slot_depth), "expert", split_axis=0, concat_axis=0, tiled=True
    ).reshape(-1)
    usable = requested >= 0
    safe_idx = jnp.maximum(requested, 0)
    gate_cols = w_gate[0]
    up_cols = w_up[0]
    down_rows = w_down[0]
    row_block = jnp.where(
        usable[:, None], jnp.take(tokens, safe_idx, axis=0), jnp.zeros((), jnp.bfloat16)
    )
    slots = lax.all_to_all(
        row_block.reshape(experts_n, slot_depth, -1),
        "expert",
        split_axis=0,
        concat_axis=0,
        tiled=True,
    )
    picked = jnp.take(slots.reshape(experts_n * slot_depth, -1), slot_of, axis=0)
    portion = lax.all_gather(picked, "ffn", axis=1, tiled=True)
    gate_next = jnp.dot(portion, gate_cols, preferred_element_type=jnp.float32)
    up_next = jnp.dot(portion, up_cols, preferred_element_type=jnp.float32)
    hidden = (jax.nn.silu(gate_next) * up_next).astype(jnp.bfloat16)
    partial_value = jnp.dot(hidden, down_rows, preferred_element_type=jnp.float32)
    summed = lax.psum_scatter(
        partial_value.astype(jnp.bfloat16), "ffn", scatter_dimension=1, tiled=True
    ).astype(jnp.float32)
    contribution = (weights[:, None] * summed).astype(jnp.bfloat16)
    returned_slots = (
        jnp.zeros((experts_n * slot_depth, contribution.shape[1]), jnp.bfloat16)
        .at[slot_of]
        .set(contribution)
    )
    returned = lax.all_to_all(
        returned_slots.reshape(experts_n, slot_depth, -1),
        "expert",
        split_axis=0,
        concat_axis=0,
        tiled=True,
    )
    returned = returned.reshape(experts_n * slot_depth, -1)
    placement_map = (requested[None, :] == jnp.arange(tok_dev, dtype=jnp.int32)[:, None]).astype(
        jnp.bfloat16
    )
    mixed = jnp.dot(placement_map, returned, preferred_element_type=jnp.float32)
    return mixed.astype(jnp.bfloat16)


LANES = 128
KINDS = 15
MESH = pl.DeviceIdType.MESH
(TO_RIGHT, TO_LEFT, ON_RIGHT, ON_LEFT, ROWS_X, ROWS_CORE, ROWS_ON,
 PART_CORE, PART_X, HALF_RIGHT, HALF_LEFT, SUM_RIGHT, SUM_LEFT,
 PLAIN_RIGHT, PLAIN_LEFT) = range(KINDS)


def dot(a, b):
    return jnp.dot(a, b, preferred_element_type=jnp.float32)


def fused(ring, cap_ref, chosen_ref, gates_ref, tok_ref, wg_ref, wu_ref, wd_ref, out_ref,
          near, pick, put, live, rows, w_in, w_out, acc, hid, part_out, part_in, own_sum,
          sum_out, sum_in, far_out, half_in, edges, edge_out, edge_in, own_out,
          send_sem, recv_sem, load_sem, mate_in):
    block, width = tok_ref.shape
    listed = chosen_ref.shape[1]
    half = block // 2
    chunks = width // LANES
    z = lax.axis_index("expert")
    f = lax.axis_index("ffn")

    def member(p):
        return p + (p // 2) * (2 * ring - 3 - 2 * p)

    spot = member(z)
    right = {"expert": member(lax.rem(spot + 1, ring))}
    left = {"expert": member(lax.rem(spot + ring - 1, ring))}
    chip, core = f // 2, f % 2
    slot_id = (f, chip * 2 + 1 - core, (1 - chip) * 2 + core, (1 - chip) * 2 + 1 - core)
    mate = {"ffn": slot_id[1]}
    across = {"ffn": slot_id[2]}

    loads = []
    ff = wg_ref.shape[1]
    for s in range(4):
        at = pl.ds(pl.multiple_of(slot_id[s] * width, width), width)
        loads.append([
            pltpu.make_async_copy(wg_ref.at[at, :], w_in.at[s, :, 0:ff], load_sem.at[3 * s]),
            pltpu.make_async_copy(wu_ref.at[at, :], w_in.at[s, :, ff:2 * ff], load_sem.at[3 * s + 1]),
            pltpu.make_async_copy(wd_ref.at[:, at], w_out.at[s], load_sem.at[3 * s + 2]),
        ])
    for group in loads:
        for load in group:
            load.start()

    barrier = pltpu.get_barrier_semaphore()
    for other in (left, right, across):
        pl.semaphore_signal(barrier, inc=1, device_id=other, device_id_type=MESH)

    @pl.when(core == 0)
    def _():
        pl.semaphore_signal(barrier, inc=1, device_id=mate, device_id_type=MESH)

    @pl.when(core == 0)
    def _():
        pl.semaphore_wait(barrier, 3)

    @pl.when(core == 1)
    def _():
        pl.semaphore_wait(barrier, 4)
        pl.semaphore_signal(mate_in, inc=1, device_id=mate, device_id_type=MESH)

    def cols(q):
        return slice(q * LANES, (q + 1) * LANES)

    def copy(kind, q):
        src, dst, to = {
            TO_RIGHT: lambda: (tok_ref.at[:, cols(q)], near.at[q, 0:block], right),
            TO_LEFT: lambda: (tok_ref.at[:, cols(q)], near.at[q, 2 * block:3 * block], left),
            ON_RIGHT: lambda: (near.at[q, 0:half], near.at[q, block:block + half], right),
            ON_LEFT: lambda: (near.at[q, 2 * block + half:3 * block], near.at[q, block + half:2 * block], left),
            ROWS_X: lambda: (rows.at[0, q], rows.at[2, q], across),
            ROWS_CORE: lambda: (rows.at[0, q], rows.at[1, q], mate),
            ROWS_ON: lambda: (rows.at[2, q], rows.at[3, q], mate),
            PART_CORE: lambda: (part_out.at[q], part_in.at[q], mate),
            PART_X: lambda: (sum_out.at[q], sum_in.at[q], across),
            HALF_RIGHT: lambda: (far_out.at[q, 0:half], half_in.at[q, 0:half], right),
            HALF_LEFT: lambda: (far_out.at[q, half:block], half_in.at[q, half:block], left),
            SUM_RIGHT: lambda: (edge_out.at[q, 0, 0:half], edge_in.at[q, 0, 0:half], right),
            SUM_LEFT: lambda: (edge_out.at[q, 1, half:block], edge_in.at[q, 1, half:block], left),
            PLAIN_RIGHT: lambda: (edge_out.at[q, 0, half:block], edge_in.at[q, 0, half:block], right),
            PLAIN_LEFT: lambda: (edge_out.at[q, 1, 0:half], edge_in.at[q, 1, 0:half], left),
        }[kind]()
        i = kind * chunks + q
        return pltpu.make_async_remote_copy(
            src_ref=src, dst_ref=dst, send_sem=send_sem.at[i], recv_sem=recv_sem.at[i],
            device_id=to, device_id_type=MESH)

    def start(kind, q):
        copy(kind, q).start()

    def got(kind, q):
        copy(kind, q).wait_recv()

    def own(q):
        start(TO_RIGHT, q)
        start(TO_LEFT, q)

    for q in range(min(2, chunks)):
        own(q)

    ids = chosen_ref[...]

    def mark():
        ids_col = jnp.broadcast_to(ids.astype(jnp.float32), (LANES, listed)).T.astype(jnp.int32)
        lane = lax.broadcasted_iota(jnp.int32, (listed, LANES), 1)
        for r in range(4):
            base = member(lax.rem(spot + ring - r, ring)) * block
            for h in range(block // LANES):
                hit = ids_col == lane + (base + h * LANES)
                pick[:, r * block + h * LANES:r * block + (h + 1) * LANES] = jnp.where(hit, 1.0, 0.0).astype(jnp.bfloat16)

    def select(q):
        got(ON_RIGHT, q)
        got(ON_LEFT, q)
        chosen_rows = dot(pick[:, 0:block], tok_ref[:, cols(q)]) + dot(pick[:, block:], near[q])
        rows[0, q] = chosen_rows.astype(jnp.bfloat16)
        start(ROWS_X, q)

    for q in range(chunks):
        got(TO_RIGHT, q)
        start(ON_RIGHT, q)
        got(TO_LEFT, q)
        start(ON_LEFT, q)
        if q + 2 < chunks:
            own(q + 2)
        if q == 0:
            mark()
        else:
            select(q - 1)
    select(chunks - 1)

    @pl.when(core == 0)
    def _():
        pl.semaphore_wait(mate_in, 1)

    for q in range(chunks):
        start(ROWS_CORE, q)

    token = lax.broadcasted_iota(jnp.int32, (block, listed), 0)
    for r in range(4):
        base = member(lax.rem(spot + ring - r, ring)) * block
        put[r] = jnp.where(ids == token + base, 1.0, 0.0).astype(jnp.bfloat16)
    position = lax.broadcasted_iota(jnp.int32, (1, listed), 1)
    kept = jnp.where(position < cap_ref[0], gates_ref[...], 0.0)
    live[...] = jnp.broadcast_to(kept, (LANES, listed)).T

    for group in loads:
        for load in group:
            load.wait()

    def whole(s):
        return jnp.concatenate([rows[s, q] for q in range(chunks)], axis=1)

    acc[...] = dot(whole(0), w_in[0])
    for q in range(chunks):
        got(ROWS_CORE, q)
    acc[...] += dot(whole(1), w_in[1])

    def add(s, q):
        acc[...] += dot(rows[s, q], w_in[s, q * LANES:(q + 1) * LANES])

    for q in range(chunks):
        got(ROWS_X, q)
        start(ROWS_ON, q)
        add(2, q)
        if q >= 1:
            got(ROWS_ON, q - 1)
            add(3, q - 1)
    got(ROWS_ON, chunks - 1)
    add(3, chunks - 1)

    gate = acc[:, 0:ff]
    hid[...] = (gate / (1.0 + jnp.exp(-gate)) * acc[:, ff:2 * ff]).astype(jnp.bfloat16)

    for q in range(chunks):
        both = jnp.concatenate([w_out[1, :, cols(q)], w_out[3, :, cols(q)]], axis=1)
        part_out[q] = dot(hid[...], both).astype(jnp.bfloat16)
        start(PART_CORE, q)
    for q in range(chunks):
        both = dot(hid[...], jnp.concatenate([w_out[0, :, cols(q)], w_out[2, :, cols(q)]], axis=1))
        got(PART_CORE, q)
        both = both + part_in[q].astype(jnp.float32)
        sum_out[q] = both[:, LANES:].astype(jnp.bfloat16)
        start(PART_X, q)
        own_sum[q] = both[:, :LANES]

    def finish(q):
        got(SUM_RIGHT, q)
        got(SUM_LEFT, q)
        got(PLAIN_RIGHT, q)
        got(PLAIN_LEFT, q)
        total = own_out[q] + edge_in[q, 0].astype(jnp.float32) + edge_in[q, 1].astype(jnp.float32)
        out_ref[:, cols(q)] = total.astype(jnp.bfloat16)

    def spread(q):
        got(PART_X, q)
        y = own_sum[q] + sum_in[q].astype(jnp.float32)
        weighted = (live[...] * y).astype(jnp.bfloat16)
        far_out[q] = dot(put[2], weighted).astype(jnp.bfloat16)
        start(HALF_RIGHT, q)
        start(HALF_LEFT, q)
        to_right = dot(put[3], weighted)
        to_left = dot(put[1], weighted)
        edge_out[q, 0, half:block] = to_right[half:block].astype(jnp.bfloat16)
        edge_out[q, 1, 0:half] = to_left[0:half].astype(jnp.bfloat16)
        start(PLAIN_RIGHT, q)
        start(PLAIN_LEFT, q)
        edges[q, 0] = to_right[0:half]
        edges[q, 1] = to_left[half:block]
        own_out[q] = dot(put[0], weighted)

    def merge(q):
        got(HALF_RIGHT, q)
        edge_out[q, 0, 0:half] = (edges[q, 0] + half_in[q, 0:half].astype(jnp.float32)).astype(jnp.bfloat16)
        start(SUM_RIGHT, q)
        got(HALF_LEFT, q)
        edge_out[q, 1, half:block] = (edges[q, 1] + half_in[q, half:block].astype(jnp.float32)).astype(jnp.bfloat16)
        start(SUM_LEFT, q)

    for q in range(chunks + 2):
        if q < chunks:
            spread(q)
        if 1 <= q <= chunks:
            merge(q - 1)
        if q >= 2:
            finish(q - 2)

    for kind in range(KINDS):
        for q in range(chunks):
            copy(kind, q).wait_send()


def shards_fused(ring, tokens, chosen, gates, capacity, w_gate, w_up, w_down):
    block, width = tokens.shape
    listed = chosen.shape[1]
    ff = w_gate.shape[2]
    chunks = width // LANES
    bf16, f32 = jnp.bfloat16, jnp.float32
    vmem = pl.BlockSpec(memory_space=pltpu.VMEM)
    far = pl.BlockSpec(memory_space=pl.ANY)
    return pl.pallas_call(
        functools.partial(fused, ring),
        out_shape=jax.ShapeDtypeStruct(tokens.shape, bf16),
        in_specs=[pl.BlockSpec(memory_space=pltpu.SMEM), vmem, vmem, vmem, far, far, far],
        out_specs=vmem,
        scratch_shapes=[
            pltpu.VMEM((chunks, 3 * block, LANES), bf16),
            pltpu.VMEM((listed, 4 * block), bf16),
            pltpu.VMEM((4, block, listed), bf16),
            pltpu.VMEM((listed, LANES), f32),
            pltpu.VMEM((4, chunks, listed, LANES), bf16),
            pltpu.VMEM((4, width, 2 * ff), bf16),
            pltpu.VMEM((4, ff, width), bf16),
            pltpu.VMEM((listed, 2 * ff), f32),
            pltpu.VMEM((listed, ff), bf16),
            pltpu.VMEM((chunks, listed, 2 * LANES), bf16),
            pltpu.VMEM((chunks, listed, 2 * LANES), bf16),
            pltpu.VMEM((chunks, listed, LANES), f32),
            pltpu.VMEM((chunks, listed, LANES), bf16),
            pltpu.VMEM((chunks, listed, LANES), bf16),
            pltpu.VMEM((chunks, block, LANES), bf16),
            pltpu.VMEM((chunks, block, LANES), bf16),
            pltpu.VMEM((chunks, 2, block // 2, LANES), f32),
            pltpu.VMEM((chunks, 2, block, LANES), bf16),
            pltpu.VMEM((chunks, 2, block, LANES), bf16),
            pltpu.VMEM((chunks, block, LANES), f32),
            pltpu.SemaphoreType.DMA((KINDS * chunks,)),
            pltpu.SemaphoreType.DMA((KINDS * chunks,)),
            pltpu.SemaphoreType.DMA((12,)),
            pltpu.SemaphoreType.REGULAR,
        ],
        compiler_params=pltpu.CompilerParams(collective_id=0, has_side_effects=True),
    )(capacity, chosen, gates, tokens, w_gate[0], w_up[0], w_down[0])


def solution(mesh):
    in_specs = (
        P(("cfg", "expert"), "ffn"),
        P(("cfg", "expert"), None),
        P(("cfg", "expert"), None),
        P("cfg"),
        P("expert", None, "ffn"),
        P("expert", None, "ffn"),
        P("expert", "ffn", None),
    )
    out_specs = P(("cfg", "expert"), "ffn")
    ring = mesh.shape["expert"]
    small = ring == 4 and mesh.shape["ffn"] == 4
    body = functools.partial(shards_fused, ring) if small else shards_general
    return jax.shard_map(body, mesh=mesh, in_specs=in_specs, out_specs=out_specs, check_vma=False)
```

profile of v0, /device:TPU:0, one launch (start us, length us, event | category | flops | bytes accessed | tf_op | source)
XLA Modules:
  0.0 62.1 jit_solution(13272272986971277644)
XLA Ops:
  0.7 59.7 %shard_map.73 = bf16[256,512]{1,0:T(8,128)(2,1)} custom-call(s32[1]{0:T(128)S(6)} %copy.9.cap_ref, s32[1,512]{1,0:T(1,128)} %chosen_ref.1, f32[1,512]{1,0:T(1,128)} %gates_ref.1, bf16[256,512]{1,0:T(8,128)(2,1)} %tok_ref.1, bf16[2048,256]{1,0:T(8,128)(2,1)} %bitcast.3, bf16[2048,256]{1,0:T(8,128)(2,1)} %bitcast.4, bf16[256,2048]{1,0:T(8,128)(2,1)} %bitcast.5), custom_call_target="tpu_custom_call" | custom-call | tf_op jit(solution)/shard_map/pallas_call | solution.py:319
  60.4 1.7 %copy.10 = bf16[256,512]{1,0:T(8,128)(2,1)} copy(bf16[256,512]{1,0:T(8,128)(2,1)} %shard_map.73) | data formatting | bytes 524288
where the time goes:
time: 62.2 us; the launch traced here: 62.1 us
  Pallas kernels  59.7 us (96%)
  local copies, waits for them, and re-layouts  1.67 us (3%)
  between operations  0.66 us (1%)
    pallas_call x1, Pallas kernels, shards_fused(): pl.pallas_call(functools.partial(fused, ring), out_shape=jax.ShapeDtypeSt...  59.7 us
    unnamed x1, local copies, waits for them, and re-layouts  1.67 us

commit v1 on v0

v1 whole, which is shorter than its diff:
```python
import jax
import jax.numpy as jnp
from jax import lax
from jax.experimental import pallas as pl
from jax.experimental.pallas import tpu as pltpu
from jax.sharding import PartitionSpec as P


def shards_general(tokens, chosen, gates, capacity, w_gate, w_up, w_down):
    experts_n = lax.axis_size("expert")
    tok_dev = tokens.shape[0]
    picked_ids = chosen[0]
    listed = picked_ids.shape[0]
    slot_depth = 2 * listed // experts_n
    positions = jnp.arange(listed, dtype=jnp.int32)
    alive_mask = positions < capacity[0]
    weights = jnp.where(alive_mask, gates[0], jnp.zeros_like(gates[0]))
    source = picked_ids // tok_dev
    offset = picked_ids - source * tok_dev
    member = (source[:, None] == jnp.arange(experts_n, dtype=jnp.int32)[None, :]).astype(jnp.int32)
    before = jnp.cumsum(member, axis=0) - member
    rank_in = jnp.sum(before * member, axis=1)
    slot_of = source * slot_depth + rank_in
    wanted = jnp.where(alive_mask, offset, -1)
    request = jnp.full((experts_n * slot_depth,), -1, jnp.int32).at[slot_of].set(wanted)
    requested = lax.all_to_all(
        request.reshape(experts_n, slot_depth), "expert", split_axis=0, concat_axis=0, tiled=True
    ).reshape(-1)
    usable = requested >= 0
    safe_idx = jnp.maximum(requested, 0)
    gate_cols = w_gate[0]
    up_cols = w_up[0]
    down_rows = w_down[0]
    row_block = jnp.where(
        usable[:, None], jnp.take(tokens, safe_idx, axis=0), jnp.zeros((), jnp.bfloat16)
    )
    slots = lax.all_to_all(
        row_block.reshape(experts_n, slot_depth, -1),
        "expert",
        split_axis=0,
        concat_axis=0,
        tiled=True,
    )
    picked = jnp.take(slots.reshape(experts_n * slot_depth, -1), slot_of, axis=0)
    portion = lax.all_gather(picked, "ffn", axis=1, tiled=True)
    gate_next = jnp.dot(portion, gate_cols, preferred_element_type=jnp.float32)
    up_next = jnp.dot(portion, up_cols, preferred_element_type=jnp.float32)
    hidden = (jax.nn.silu(gate_next) * up_next).astype(jnp.bfloat16)
    partial_value = jnp.dot(hidden, down_rows, preferred_element_type=jnp.float32)
    summed = lax.psum_scatter(
        partial_value.astype(jnp.bfloat16), "ffn", scatter_dimension=1, tiled=True
    ).astype(jnp.float32)
    contribution = (weights[:, None] * summed).astype(jnp.bfloat16)
    returned_slots = (
        jnp.zeros((experts_n * slot_depth, contribution.shape[1]), jnp.bfloat16)
        .at[slot_of]
        .set(contribution)
    )
    returned = lax.all_to_all(
        returned_slots.reshape(experts_n, slot_depth, -1),
        "expert",
        split_axis=0,
        concat_axis=0,
        tiled=True,
    )
    returned = returned.reshape(experts_n * slot_depth, -1)
    placement_map = (requested[None, :] == jnp.arange(tok_dev, dtype=jnp.int32)[:, None]).astype(
        jnp.bfloat16
    )
    mixed = jnp.dot(placement_map, returned, preferred_element_type=jnp.float32)
    return mixed.astype(jnp.bfloat16)


LANES = 128
PLAIN = 2
MESH = pl.DeviceIdType.MESH
KINDS = 20
(D_PAIR, D_PEER, D_CROSS, F_PEER, F_FAR, MERGED_A, MERGED_B, X_SAME, X_DIAG, X_MATE,
 Y_SAME, Y_DIAG, Y_MATE, C_PAIR, P_PAIR, P_CROSS, P_PEER, W_IN, W_OUT, IDS) = range(KINDS)


def dot(a, b):
    return jnp.dot(a, b, preferred_element_type=jnp.float32)


def fused(cap_ref, chosen_ref, gates_ref, tok_hbm, wg_ref, wu_ref, wd_ref, out_ref,
          tok, near, pick, pick_pair, put, put_pair, live, ids_pair, rows, merged, merged_in,
          x_in, x_mate, w_in, w_in_mate, w_out, w_out_mate, acc, hid, y_out, y_in, own_sum,
          con, con_in, part_pair, part_cross, part_peer, part_in, own_out,
          send_sem, recv_sem, load_sem):
    block, width = tok.shape
    listed = chosen_ref.shape[1]
    half = listed // 2
    chunks = width // LANES
    ff = wg_ref.shape[1]
    bf16, f32 = jnp.bfloat16, jnp.float32
    z = lax.axis_index("expert")
    f = lax.axis_index("ffn")
    inner = ((z + 1) // 2) % 2
    pair = z + 1 - 2 * (z % 2)
    mirror = 3 - z
    cross = z + 2 - 4 * (z // 2)
    chip, core = f // 2, f % 2
    slot_id = (f, chip * 2 + 1 - core, (1 - chip) * 2 + core, (1 - chip) * 2 + 1 - core)
    mate, same, diag = ({"ffn": slot_id[s]} for s in (1, 2, 3))
    to_pair, to_mirror, to_cross = ({"expert": e} for e in (pair, mirror, cross))
    sources = (z, pair, cross + (mirror - cross) * inner, mirror + (cross - mirror) * inner)

    barrier = pltpu.get_barrier_semaphore()
    for other in (to_pair, to_cross, mate, same, diag):
        pl.semaphore_signal(barrier, inc=1, device_id=other, device_id_type=MESH)

    @pl.when(inner == 1)
    def _():
        pl.semaphore_signal(barrier, inc=1, device_id=to_mirror, device_id_type=MESH)

    def cols(q):
        return slice(q * LANES, (q + 1) * LANES)

    tok_loads = [pltpu.make_async_copy(tok_hbm.at[:, cols(q)], tok.at[:, cols(q)], load_sem.at[12 + q])
                 for q in range(chunks)]
    for load in tok_loads:
        load.start()
    loads = []
    for s in range(4):
        at = pl.ds(pl.multiple_of(slot_id[s] * width, width), width)
        loads.append([
            pltpu.make_async_copy(wg_ref.at[at, :], w_in.at[s, :, 0:ff], load_sem.at[3 * s]),
            pltpu.make_async_copy(wu_ref.at[at, :], w_in.at[s, :, ff:2 * ff], load_sem.at[3 * s + 1]),
            pltpu.make_async_copy(wd_ref.at[:, at], w_out.at[s], load_sem.at[3 * s + 2]),
        ])
    for group in loads:
        for load in group:
            load.start()

    def copy(kind, q):
        first, second = slice(0, half), slice(half, listed)
        src, dst, to = {
            D_PAIR: lambda: (tok.at[:, cols(q)], near.at[q, 0:block], to_pair),
            D_PEER: lambda: (tok.at[:, cols(q)], near.at[q, block:2 * block], to_mirror),
            D_CROSS: lambda: (tok.at[:, cols(q)], near.at[q, 2 * block:3 * block], to_cross),
            F_PEER: lambda: (near.at[q, block:2 * block], near.at[q, block:2 * block], to_pair),
            F_FAR: lambda: (near.at[q, 2 * block:3 * block], near.at[q, 2 * block:3 * block], to_pair),
            MERGED_A: lambda: (merged.at[q, first], merged_in.at[q, first], to_pair),
            MERGED_B: lambda: (merged.at[q, second], merged_in.at[q, second], to_pair),
            X_SAME: lambda: (rows.at[q, first], x_in.at[0, q], same),
            X_DIAG: lambda: (rows.at[q, second], x_in.at[1, q], diag),
            X_MATE: lambda: (rows.at[q, second], x_mate.at[q], mate),
            Y_SAME: lambda: (y_out.at[0, q], y_in.at[0, q], same),
            Y_DIAG: lambda: (y_out.at[1, q], y_in.at[1, q], diag),
            Y_MATE: lambda: (y_out.at[2, q], y_in.at[2, q], mate),
            C_PAIR: lambda: (con.at[q], con_in.at[q], to_pair),
            P_PAIR: lambda: (part_pair.at[q], part_in.at[0, q], to_pair),
            P_CROSS: lambda: (part_cross.at[q], part_in.at[1, q], to_cross),
            P_PEER: lambda: (part_peer.at[q], part_in.at[0, q], to_mirror),
            W_IN: lambda: (w_in.at[q], w_in_mate.at[q ^ 1], mate),
            W_OUT: lambda: (w_out.at[q], w_out_mate.at[q ^ 1], mate),
            IDS: lambda: (chosen_ref, ids_pair, to_pair),
        }[kind]()
        sent = kind * chunks + q
        landed = kind * chunks + (q ^ 1 if kind in (W_IN, W_OUT) else q)
        return pltpu.make_async_remote_copy(
            src_ref=src, dst_ref=dst, send_sem=send_sem.at[sent], recv_sem=recv_sem.at[landed],
            device_id=to, device_id_type=MESH)

    def start(kind, q):
        copy(kind, q).start()

    def got(kind, q):
        copy(kind, q ^ 1 if kind in (W_IN, W_OUT) else q).wait_recv()

    pl.semaphore_wait(barrier, 5 + inner)

    @pl.when(inner == 0)
    def _():
        start(IDS, 0)
        for q in range(chunks):
            tok_loads[q].wait()
            start(D_CROSS, q)
            start(D_PAIR, q)

    @pl.when(inner == 1)
    def _():
        for q in range(chunks):
            tok_loads[q].wait()
            start(D_PEER, q)
            if q < PLAIN:
                start(D_PAIR, q)

    for group in loads:
        for load in group:
            load.wait()
    for s in range(4):
        start(W_IN, s)
    for s in range(4):
        start(W_OUT, s)

    def turned(value):
        other = jnp.concatenate([value[:, half:], value[:, :half]], axis=1)
        return jnp.where(core == 1, other, value)

    def column(ids):
        return jnp.broadcast_to(ids.astype(f32), (LANES, listed)).T.astype(jnp.int32)

    lane = lax.broadcasted_iota(jnp.int32, (listed, LANES), 1)
    token = lax.broadcasted_iota(jnp.int32, (block, listed), 0)

    def mark(dst, ids, blocks):
        ids_col = column(ids)
        for r, source in enumerate(blocks):
            for h in range(block // LANES):
                hit = ids_col == lane + (source * block + h * LANES)
                at = r * block + h * LANES
                dst[:, at:at + LANES] = jnp.where(hit, 1.0, 0.0).astype(bf16)

    def mark_rows(dst, ids, blocks):
        for r, source in enumerate(blocks):
            dst[r] = jnp.where(ids == token + source * block, 1.0, 0.0).astype(bf16)

    ids = turned(chosen_ref[...])
    mark(pick, ids, sources)
    mark_rows(put, ids, sources)
    position = turned(lax.broadcasted_iota(jnp.int32, (1, listed), 1))
    kept = jnp.where(position < cap_ref[0], turned(gates_ref[...]), 0.0)
    live[...] = jnp.broadcast_to(kept, (LANES, listed)).T

    def picked(matrix, q, part, has_pair):
        at = slice(part * half, (part + 1) * half)
        low = 0 if has_pair else block
        return dot(matrix[at, 0:block], tok[:, cols(q)]) + dot(matrix[at, block:], near[q, low:])

    def send_rows(q, first, second):
        rows[q, 0:half] = first().astype(bf16)
        start(X_SAME, q)
        rows[q, half:listed] = second().astype(bf16)
        start(X_DIAG, q)
        start(X_MATE, q)

    def add(q, pieces, slots, begin=False):
        at = slice(q * LANES, (q + 1) * LANES)
        lhs = jnp.concatenate(pieces, axis=1)
        for i, w in enumerate((w_in, w_in_mate)):
            rhs = jnp.concatenate([w[s, at] for s in slots], axis=0)
            out = slice(i * 2 * ff, (i + 1) * 2 * ff)
            if begin:
                acc[:, out] = dot(lhs, rhs)
            else:
                acc[:, out] += dot(lhs, rhs)

    def add_chip(q):
        got(X_MATE, q)
        if q == 0:
            for s in range(4):
                got(W_IN, s)
        add(q, [rows[q, 0:half], x_mate[q]], (0, 1), q == 0)

    def add_across(q):
        got(X_SAME, q)
        got(X_DIAG, q)
        add(q, [x_in[0, q], x_in[1, q]], (2, 3))

    def behind(q):
        if q >= 1:
            add_chip(q - 1)
        if q >= 2:
            add_across(q - 2)

    @pl.when(inner == 1)
    def _():
        got(IDS, 0)
        pair_ids = turned(ids_pair[...])
        mark(pick_pair, pair_ids, (sources[0],) + sources[2:])
        mark_rows(put_pair, pair_ids, (sources[0],) + sources[2:])
        for q in range(chunks):
            got(D_PEER, q)
            if q < PLAIN:
                start(F_PEER, q)
            got(D_CROSS, q)
            if q < PLAIN:
                start(F_FAR, q)
            else:
                for part, kind in ((0, MERGED_A), (1, MERGED_B)):
                    at = slice(part * half, (part + 1) * half)
                    merged[q, at] = picked(pick_pair, q, part, False).astype(bf16)
                    start(kind, q)
            got(D_PAIR, q)
            send_rows(q, lambda: picked(pick, q, 0, True), lambda: picked(pick, q, 1, True))
            behind(q)

    @pl.when(inner == 0)
    def _():
        for q in range(chunks):
            if q < PLAIN:
                got(D_PAIR, q)
                got(F_PEER, q)
                got(F_FAR, q)
                send_rows(q, lambda: picked(pick, q, 0, True), lambda: picked(pick, q, 1, True))
            else:
                def from_pair(part, kind):
                    at = slice(part * half, (part + 1) * half)
                    own = dot(pick[at, 0:block], tok[:, cols(q)])
                    got(kind, q)
                    return own + merged_in[q, at].astype(f32)

                send_rows(q, lambda: from_pair(0, MERGED_A), lambda: from_pair(1, MERGED_B))
            behind(q)

    add_chip(chunks - 1)
    for q in range(max(chunks - 2, 0), chunks):
        add_across(q)

    for i in range(2):
        gate = acc[:, i * 2 * ff:i * 2 * ff + ff]
        up = acc[:, i * 2 * ff + ff:(i + 1) * 2 * ff]
        hid[i] = (gate / (1.0 + jnp.exp(-gate)) * up).astype(bf16)

    def down(q, slots):
        total = None
        for i, w in enumerate((w_out, w_out_mate)):
            part = dot(hid[i], jnp.concatenate([w[s, :, cols(q)] for s in slots], axis=1))
            total = part if total is None else total + part
        return total[:, :LANES], total[:, LANES:]

    for s in range(4):
        got(W_OUT, s)
    for q in range(chunks):
        first, second = down(q, (2, 3))
        y_out[0, q] = first.astype(bf16)
        start(Y_SAME, q)
        y_out[1, q] = second.astype(bf16)
        start(Y_DIAG, q)
    for q in range(chunks):
        first, second = down(q, (0, 1))
        own_sum[q] = first
        y_out[2, q] = second.astype(bf16)
        start(Y_MATE, q)

    def weigh(q):
        got(Y_MATE, q)
        got(Y_SAME, q)
        con[q, 0:half] = (live[0:half] * (own_sum[q] + y_in[0, q].astype(f32))).astype(bf16)
        got(Y_DIAG, q)
        other = y_in[2, q].astype(f32) + y_in[1, q].astype(f32)
        con[q, half:listed] = (live[half:listed] * other).astype(bf16)

    @pl.when(inner == 0)
    def _():
        for q in range(chunks):
            weigh(q)
            start(C_PAIR, q)
            own_out[q] = dot(put[0], con[q])
        for q in range(chunks):
            got(P_PAIR, q)
            got(P_CROSS, q)
            total = own_out[q] + part_in[0, q].astype(f32) + part_in[1, q].astype(f32)
            out_ref[:, cols(q)] = total.astype(bf16)

    @pl.when(inner == 1)
    def _():
        for q in range(chunks):
            weigh(q)
            part_pair[q] = dot(put[1], con[q]).astype(bf16)
            start(P_PAIR, q)
        for q in range(chunks):
            got(C_PAIR, q)
            part_cross[q] = (dot(put[3], con[q]) + dot(put_pair[2], con_in[q])).astype(bf16)
            start(P_CROSS, q)
            part_peer[q] = (dot(put[2], con[q]) + dot(put_pair[1], con_in[q])).astype(bf16)
            start(P_PEER, q)
            own_out[q] = dot(put[0], con[q]) + dot(put_pair[0], con_in[q])
        for q in range(chunks):
            got(P_PEER, q)
            total = own_out[q] + part_in[0, q].astype(f32)
            out_ref[:, cols(q)] = total.astype(bf16)

    def sent(kind, q):
        copy(kind, q).wait_send()

    for q in range(chunks):
        for kind in (X_SAME, X_DIAG, X_MATE, Y_SAME, Y_DIAG, Y_MATE):
            sent(kind, q)
    for s in range(4):
        sent(W_IN, s)
        sent(W_OUT, s)

    @pl.when(inner == 0)
    def _():
        sent(IDS, 0)
        for q in range(chunks):
            for kind in (D_CROSS, D_PAIR, C_PAIR):
                sent(kind, q)

    @pl.when(inner == 1)
    def _():
        for q in range(chunks):
            for kind in (D_PEER, P_PAIR, P_CROSS, P_PEER):
                sent(kind, q)
            for kind in (D_PAIR, F_PEER, F_FAR) if q < PLAIN else (MERGED_A, MERGED_B):
                sent(kind, q)


def shards_fused(tokens, chosen, gates, capacity, w_gate, w_up, w_down):
    block, width = tokens.shape
    listed = chosen.shape[1]
    half = listed // 2
    ff = w_gate.shape[2]
    chunks = width // LANES
    bf16, f32 = jnp.bfloat16, jnp.float32
    vmem = pl.BlockSpec(memory_space=pltpu.VMEM)
    far = pl.BlockSpec(memory_space=pl.ANY)
    return pl.pallas_call(
        fused,
        out_shape=jax.ShapeDtypeStruct(tokens.shape, bf16),
        in_specs=[pl.BlockSpec(memory_space=pltpu.SMEM), vmem, vmem, far, far, far, far],
        out_specs=vmem,
        scratch_shapes=[
            pltpu.VMEM((block, width), bf16),
            pltpu.VMEM((chunks, 3 * block, LANES), bf16),
            pltpu.VMEM((listed, 4 * block), bf16),
            pltpu.VMEM((listed, 3 * block), bf16),
            pltpu.VMEM((4, block, listed), bf16),
            pltpu.VMEM((3, block, listed), bf16),
            pltpu.VMEM((listed, LANES), f32),
            pltpu.VMEM((1, listed), jnp.int32),
            pltpu.VMEM((chunks, listed, LANES), bf16),
            pltpu.VMEM((chunks, listed, LANES), bf16),
            pltpu.VMEM((chunks, listed, LANES), bf16),
            pltpu.VMEM((2, chunks, half, LANES), bf16),
            pltpu.VMEM((chunks, half, LANES), bf16),
            pltpu.VMEM((4, width, 2 * ff), bf16),
            pltpu.VMEM((4, width, 2 * ff), bf16),
            pltpu.VMEM((4, ff, width), bf16),
            pltpu.VMEM((4, ff, width), bf16),
            pltpu.VMEM((half, 4 * ff), f32),
            pltpu.VMEM((2, half, ff), bf16),
            pltpu.VMEM((3, chunks, half, LANES), bf16),
            pltpu.VMEM((3, chunks, half, LANES), bf16),
            pltpu.VMEM((chunks, half, LANES), f32),
            pltpu.VMEM((chunks, listed, LANES), bf16),
            pltpu.VMEM((chunks, listed, LANES), bf16),
            pltpu.VMEM((chunks, block, LANES), bf16),
            pltpu.VMEM((chunks, block, LANES), bf16),
            pltpu.VMEM((chunks, block, LANES), bf16),
            pltpu.VMEM((2, chunks, block, LANES), bf16),
            pltpu.VMEM((chunks, block, LANES), f32),
            pltpu.SemaphoreType.DMA((KINDS * chunks,)),
            pltpu.SemaphoreType.DMA((KINDS * chunks,)),
            pltpu.SemaphoreType.DMA((12 + chunks,)),
        ],
        compiler_params=pltpu.CompilerParams(collective_id=0, has_side_effects=True),
    )(capacity, chosen, gates, tokens, w_gate[0], w_up[0], w_down[0])


def solution(mesh):
    in_specs = (
        P(("cfg", "expert"), "ffn"),
        P(("cfg", "expert"), None),
        P(("cfg", "expert"), None),
        P("cfg"),
        P("expert", None, "ffn"),
        P("expert", None, "ffn"),
        P("expert", "ffn", None),
    )
    out_specs = P(("cfg", "expert"), "ffn")
    small = mesh.shape["expert"] == 4 and mesh.shape["ffn"] == 4
    body = shards_fused if small else shards_general
    return jax.shard_map(body, mesh=mesh, in_specs=in_specs, out_specs=out_specs, check_vma=False)
```

time: 62.2 us -> 55.5 us (0.89)
  Pallas kernels: 59.7 us -> 53 us
    pallas_call x1, Pallas kernels: 59.7 us -> 53 us  [shards_fused(): pl.pallas_call(fused, out_shape=jax.ShapeDtypeStruct(tokens.shape, bf16),...]
where the time goes in v1:
time: 55.5 us; the launch traced here: 55.3 us
  Pallas kernels  53 us (95%)
  local copies, waits for them, and re-layouts  1.67 us (3%)
  between operations  0.66 us (1%)
    pallas_call x1, Pallas kernels, shards_fused(): pl.pallas_call(fused, out_shape=jax.ShapeDtypeStruct(tokens.shape, bf16),...  53 us
    unnamed x1, local copies, waits for them, and re-layouts  1.67 us

profile of v1, /device:TPU:0, one launch (start us, length us, event | category | flops | bytes accessed | tf_op | source)
XLA Modules:
  0.0 55.3 jit_solution(3809984747150948992)
XLA Ops:
  0.7 53.0 %shard_map.73 = bf16[256,512]{1,0:T(8,128)(2,1)} custom-call(s32[1]{0:T(128)S(6)} %copy.9.cap_ref, s32[1,512]{1,0:T(1,128)} %chosen_ref.1, f32[1,512]{1,0:T(1,128)} %gates_ref.1, bf16[256,512]{1,0:T(8,128)(2,1)} %tok_hbm.1, bf16[2048,256]{1,0:T(8,128)(2,1)} %bitcast.3, bf16[2048,256]{1,0:T(8,128)(2,1)} %bitcast.4, bf16[256,2048]{1,0:T(8,128)(2,1)} %bitcast.5), custom_call_target="tpu_custom_call" | custom-call | tf_op jit(solution)/shard_map/pallas_call | solution.py:411
  53.7 1.7 %copy.10 = bf16[256,512]{1,0:T(8,128)(2,1)} copy(bf16[256,512]{1,0:T(8,128)(2,1)} %shard_map.73) | data formatting | bytes 524288

commit v2 on v1

--- a/solution.py
+++ b/solution.py
@@ -72,22 +72,25 @@
 
 
 LANES = 128
-PLAIN = 2
 MESH = pl.DeviceIdType.MESH
 KINDS = 20
-(D_PAIR, D_PEER, D_CROSS, F_PEER, F_FAR, MERGED_A, MERGED_B, X_SAME, X_DIAG, X_MATE,
- Y_SAME, Y_DIAG, Y_MATE, C_PAIR, P_PAIR, P_CROSS, P_PEER, W_IN, W_OUT, IDS) = range(KINDS)
+PIECES = 8
+DISPATCH = ("plain", "plain", "plain", "merged")
+COMBINE = ("merged", "merged", "merged", "merged")
+VMEM_BYTES = 66 * 1000 * 1000
+(D_PAIR, D_PEER, D_CROSS, D_FAR, F_PEER, F_FAR, MERGED_A, MERGED_B, X_SAME, X_DIAG, X_MATE,
+ Y_SAME, Y_DIAG, Y_MATE, C_FIRST, C_SECOND, P_PAIR, P_CROSS, P_PEER, IDS) = range(KINDS)
 
 
 def dot(a, b):
     return jnp.dot(a, b, preferred_element_type=jnp.float32)
 
 
-def fused(cap_ref, chosen_ref, gates_ref, tok_hbm, wg_ref, wu_ref, wd_ref, out_ref,
-          tok, near, pick, pick_pair, put, put_pair, live, ids_pair, rows, merged, merged_in,
+def fused(cap_hbm, chosen_hbm, gates_hbm, tok_hbm, wg_ref, wu_ref, wd_ref, out_ref,
+          cap_ref, chosen_ref, gates_ref, tok, near, pick, pick_pair, put, put_pair, live, ids_pair, rows, merged, merged_in,
           x_in, x_mate, w_in, w_in_mate, w_out, w_out_mate, acc, hid, y_out, y_in, own_sum,
           con, con_in, part_pair, part_cross, part_peer, part_in, own_out,
-          send_sem, recv_sem, load_sem):
+          send_sem, recv_sem, load_sem, w_send_sem, w_recv_sem):
     block, width = tok.shape
     listed = chosen_ref.shape[1]
     half = listed // 2
@@ -119,7 +122,9 @@
 
     tok_loads = [pltpu.make_async_copy(tok_hbm.at[:, cols(q)], tok.at[:, cols(q)], load_sem.at[12 + q])
                  for q in range(chunks)]
-    for load in tok_loads:
+    small_loads = [pltpu.make_async_copy(src, dst, load_sem.at[12 + chunks + i]) for i, (src, dst) in enumerate(
+        ((chosen_hbm, chosen_ref), (gates_hbm, gates_ref), (cap_hbm, cap_ref)))]
+    for load in small_loads[:1] + tok_loads + small_loads[1:]:
         load.start()
     loads = []
     for s in range(4):
@@ -139,6 +144,7 @@
             D_PAIR: lambda: (tok.at[:, cols(q)], near.at[q, 0:block], to_pair),
             D_PEER: lambda: (tok.at[:, cols(q)], near.at[q, block:2 * block], to_mirror),
             D_CROSS: lambda: (tok.at[:, cols(q)], near.at[q, 2 * block:3 * block], to_cross),
+            D_FAR: lambda: (tok.at[:, cols(q)], near.at[q, 2 * block:3 * block], to_mirror),
             F_PEER: lambda: (near.at[q, block:2 * block], near.at[q, block:2 * block], to_pair),
             F_FAR: lambda: (near.at[q, 2 * block:3 * block], near.at[q, 2 * block:3 * block], to_pair),
             MERGED_A: lambda: (merged.at[q, first], merged_in.at[q, first], to_pair),
@@ -149,51 +155,82 @@
             Y_SAME: lambda: (y_out.at[0, q], y_in.at[0, q], same),
             Y_DIAG: lambda: (y_out.at[1, q], y_in.at[1, q], diag),
             Y_MATE: lambda: (y_out.at[2, q], y_in.at[2, q], mate),
-            C_PAIR: lambda: (con.at[q], con_in.at[q], to_pair),
+            C_FIRST: lambda: (con.at[q, first], con_in.at[q, first], to_pair),
+            C_SECOND: lambda: (con.at[q, second], con_in.at[q, second], to_pair),
             P_PAIR: lambda: (part_pair.at[q], part_in.at[0, q], to_pair),
             P_CROSS: lambda: (part_cross.at[q], part_in.at[1, q], to_cross),
-            P_PEER: lambda: (part_peer.at[q], part_in.at[0, q], to_mirror),
-            W_IN: lambda: (w_in.at[q], w_in_mate.at[q ^ 1], mate),
-            W_OUT: lambda: (w_out.at[q], w_out_mate.at[q ^ 1], mate),
+            P_PEER: lambda: (part_peer.at[q], part_in.at[2, q], to_mirror),
             IDS: lambda: (chosen_ref, ids_pair, to_pair),
         }[kind]()
-        sent = kind * chunks + q
-        landed = kind * chunks + (q ^ 1 if kind in (W_IN, W_OUT) else q)
+        i = kind * chunks + q
         return pltpu.make_async_remote_copy(
-            src_ref=src, dst_ref=dst, send_sem=send_sem.at[sent], recv_sem=recv_sem.at[landed],
+            src_ref=src, dst_ref=dst, send_sem=send_sem.at[i], recv_sem=recv_sem.at[i],
             device_id=to, device_id_type=MESH)
+
+    def w_copy(s, q):
+        if q < chunks:
+            src, dst = w_in.at[s, cols(q)], w_in_mate.at[s ^ 1, cols(q)]
+        else:
+            src, dst = w_out.at[s], w_out_mate.at[s ^ 1]
+        return pltpu.make_async_remote_copy(
+            src_ref=src, dst_ref=dst, send_sem=w_send_sem.at[s * (chunks + 1) + q],
+            recv_sem=w_recv_sem.at[(s ^ 1) * (chunks + 1) + q], device_id=mate, device_id_type=MESH)
+
+    pieces = []
+    for q in range(chunks):
+        pieces += [(0, q), (1, q)]
+        if q >= 1:
+            pieces += [(2, q - 1), (3, q - 1)]
+    pieces += [(2, chunks - 1), (3, chunks - 1)] + [(s, chunks) for s in (2, 3, 0, 1)]
+
+    def push(left, number):
+        for s, q in left[:number]:
+            w_copy(s, q).start()
+        return left[number:]
+
+    def push_some(left):
+        return push(left, 4)
+
+    def w_got(slots, q):
+        for s in slots:
+            w_copy(s ^ 1, q).wait_recv()
 
     def start(kind, q):
         copy(kind, q).start()
 
     def got(kind, q):
-        copy(kind, q ^ 1 if kind in (W_IN, W_OUT) else q).wait_recv()
+        copy(kind, q).wait_recv()
+
+    def mode(q):
+        return DISPATCH[q]
 
     pl.semaphore_wait(barrier, 5 + inner)
 
     @pl.when(inner == 0)
     def _():
+        small_loads[0].wait()
         start(IDS, 0)
         for q in range(chunks):
             tok_loads[q].wait()
-            start(D_CROSS, q)
-            start(D_PAIR, q)
+            if mode(q) != "direct":
+                start(D_CROSS, q)
+                start(D_PAIR, q)
 
     @pl.when(inner == 1)
     def _():
         for q in range(chunks):
             tok_loads[q].wait()
             start(D_PEER, q)
-            if q < PLAIN:
+            if mode(q) != "merged":
                 start(D_PAIR, q)
+        small_loads[0].wait()
 
     for group in loads:
         for load in group:
             load.wait()
-    for s in range(4):
-        start(W_IN, s)
-    for s in range(4):
-        start(W_OUT, s)
+    for load in small_loads[1:]:
+        load.wait()
+    pieces = push(pieces, PIECES)
 
     def turned(value):
         other = jnp.concatenate([value[:, half:], value[:, :half]], axis=1)
@@ -249,14 +286,13 @@
 
     def add_chip(q):
         got(X_MATE, q)
-        if q == 0:
-            for s in range(4):
-                got(W_IN, s)
+        w_got((0, 1), q)
         add(q, [rows[q, 0:half], x_mate[q]], (0, 1), q == 0)
 
     def add_across(q):
         got(X_SAME, q)
         got(X_DIAG, q)
+        w_got((2, 3), q)
         add(q, [x_in[0, q], x_in[1, q]], (2, 3))
 
     def behind(q):
@@ -271,29 +307,38 @@
         pair_ids = turned(ids_pair[...])
         mark(pick_pair, pair_ids, (sources[0],) + sources[2:])
         mark_rows(put_pair, pair_ids, (sources[0],) + sources[2:])
+        left = pieces
         for q in range(chunks):
             got(D_PEER, q)
-            if q < PLAIN:
+            if mode(q) != "merged":
                 start(F_PEER, q)
             got(D_CROSS, q)
-            if q < PLAIN:
+            if mode(q) == "plain":
                 start(F_FAR, q)
-            else:
+            elif mode(q) == "merged":
                 for part, kind in ((0, MERGED_A), (1, MERGED_B)):
                     at = slice(part * half, (part + 1) * half)
                     merged[q, at] = picked(pick_pair, q, part, False).astype(bf16)
                     start(kind, q)
             got(D_PAIR, q)
             send_rows(q, lambda: picked(pick, q, 0, True), lambda: picked(pick, q, 1, True))
+            left = push_some(left)
             behind(q)
 
     @pl.when(inner == 0)
     def _():
-        for q in range(chunks):
-            if q < PLAIN:
+        left = pieces
+        for q in range(chunks):
+            if mode(q) != "merged":
                 got(D_PAIR, q)
+                if q == 0:
+                    for late in range(chunks):
+                        if mode(late) == "direct":
+                            start(D_FAR, late)
+                            start(D_CROSS, late)
+                            start(D_PAIR, late)
                 got(F_PEER, q)
-                got(F_FAR, q)
+                got(F_FAR if mode(q) == "plain" else D_FAR, q)
                 send_rows(q, lambda: picked(pick, q, 0, True), lambda: picked(pick, q, 1, True))
             else:
                 def from_pair(part, kind):
@@ -303,6 +348,7 @@
                     return own + merged_in[q, at].astype(f32)
 
                 send_rows(q, lambda: from_pair(0, MERGED_A), lambda: from_pair(1, MERGED_B))
+            left = push_some(left)
             behind(q)
 
     add_chip(chunks - 1)
@@ -321,57 +367,79 @@
             total = part if total is None else total + part
         return total[:, :LANES], total[:, LANES:]
 
-    for s in range(4):
-        got(W_OUT, s)
+    w_got((2, 3), chunks)
     for q in range(chunks):
         first, second = down(q, (2, 3))
         y_out[0, q] = first.astype(bf16)
         start(Y_SAME, q)
         y_out[1, q] = second.astype(bf16)
         start(Y_DIAG, q)
+    w_got((0, 1), chunks)
     for q in range(chunks):
         first, second = down(q, (0, 1))
         own_sum[q] = first
         y_out[2, q] = second.astype(bf16)
         start(Y_MATE, q)
 
-    def weigh(q):
-        got(Y_MATE, q)
+    def weigh_first(q):
         got(Y_SAME, q)
         con[q, 0:half] = (live[0:half] * (own_sum[q] + y_in[0, q].astype(f32))).astype(bf16)
+
+    def weigh_second(q):
+        got(Y_MATE, q)
         got(Y_DIAG, q)
         other = y_in[2, q].astype(f32) + y_in[1, q].astype(f32)
         con[q, half:listed] = (live[half:listed] * other).astype(bf16)
 
+    def spread(q, order):
+        for kind, part, slot in order:
+            part[q] = dot(put[slot], con[q]).astype(bf16)
+            start(kind, q)
+
+    def finish(q, kinds):
+        total = own_out[q]
+        for kind, slot in kinds:
+            got(kind, q)
+            total = total + part_in[slot, q].astype(f32)
+        out_ref[:, cols(q)] = total.astype(bf16)
+
+    every = ((P_PAIR, 0), (P_CROSS, 1), (P_PEER, 2))
+
     @pl.when(inner == 0)
     def _():
         for q in range(chunks):
-            weigh(q)
-            start(C_PAIR, q)
+            weigh_first(q)
+            if COMBINE[q] == "merged":
+                start(C_FIRST, q)
+            weigh_second(q)
+            if COMBINE[q] == "merged":
+                start(C_SECOND, q)
+            else:
+                spread(q, ((P_PEER, part_peer, 3), (P_CROSS, part_cross, 2), (P_PAIR, part_pair, 1)))
             own_out[q] = dot(put[0], con[q])
         for q in range(chunks):
-            got(P_PAIR, q)
-            got(P_CROSS, q)
-            total = own_out[q] + part_in[0, q].astype(f32) + part_in[1, q].astype(f32)
-            out_ref[:, cols(q)] = total.astype(bf16)
+            finish(q, every[:2] if COMBINE[q] == "merged" else every)
 
     @pl.when(inner == 1)
     def _():
         for q in range(chunks):
-            weigh(q)
-            part_pair[q] = dot(put[1], con[q]).astype(bf16)
-            start(P_PAIR, q)
-        for q in range(chunks):
-            got(C_PAIR, q)
-            part_cross[q] = (dot(put[3], con[q]) + dot(put_pair[2], con_in[q])).astype(bf16)
-            start(P_CROSS, q)
-            part_peer[q] = (dot(put[2], con[q]) + dot(put_pair[1], con_in[q])).astype(bf16)
-            start(P_PEER, q)
-            own_out[q] = dot(put[0], con[q]) + dot(put_pair[0], con_in[q])
-        for q in range(chunks):
-            got(P_PEER, q)
-            total = own_out[q] + part_in[0, q].astype(f32)
-            out_ref[:, cols(q)] = total.astype(bf16)
+            weigh_first(q)
+            weigh_second(q)
+            if COMBINE[q] == "merged":
+                spread(q, ((P_PAIR, part_pair, 1),))
+            else:
+                spread(q, ((P_CROSS, part_cross, 3), (P_PEER, part_peer, 2), (P_PAIR, part_pair, 1)))
+                own_out[q] = dot(put[0], con[q])
+        for q in range(chunks):
+            if COMBINE[q] == "merged":
+                got(C_FIRST, q)
+                got(C_SECOND, q)
+                for kind, part, mine, his in ((P_CROSS, part_cross, 3, 2), (P_PEER, part_peer, 2, 1)):
+                    part[q] = (dot(put[mine], con[q]) + dot(put_pair[his], con_in[q])).astype(bf16)
+                    start(kind, q)
+                own_out[q] = dot(put[0], con[q]) + dot(put_pair[0], con_in[q])
+        for q in range(chunks):
+            finish(q, every[2:] if COMBINE[q] == "merged" else every)
 
     def sent(kind, q):
         copy(kind, q).wait_send()
@@ -380,23 +448,23 @@
         for kind in (X_SAME, X_DIAG, X_MATE, Y_SAME, Y_DIAG, Y_MATE):
             sent(kind, q)
     for s in range(4):
-        sent(W_IN, s)
-        sent(W_OUT, s)
-
-    @pl.when(inner == 0)
-    def _():
-        sent(IDS, 0)
-        for q in range(chunks):
-            for kind in (D_CROSS, D_PAIR, C_PAIR):
-                sent(kind, q)
-
-    @pl.when(inner == 1)
-    def _():
-        for q in range(chunks):
-            for kind in (D_PEER, P_PAIR, P_CROSS, P_PEER):
-                sent(kind, q)
-            for kind in (D_PAIR, F_PEER, F_FAR) if q < PLAIN else (MERGED_A, MERGED_B):
-                sent(kind, q)
+        for q in range(chunks + 1):
+            w_copy(s, q).wait_send()
+
+    combined = {"merged": ((C_FIRST, C_SECOND), (P_PAIR, P_CROSS, P_PEER)),
+                "direct": ((P_PAIR, P_CROSS, P_PEER),) * 2}
+    dispatched = {"plain": ((D_CROSS, D_PAIR), (D_PEER, D_PAIR, F_PEER, F_FAR)),
+                  "merged": ((D_CROSS, D_PAIR), (D_PEER, MERGED_A, MERGED_B)),
+                  "direct": ((D_CROSS, D_PAIR, D_FAR), (D_PEER, D_PAIR, F_PEER))}
+
+    for role in range(2):
+        @pl.when(inner == role)
+        def _():
+            if role == 0:
+                sent(IDS, 0)
+            for q in range(chunks):
+                for kind in dispatched[DISPATCH[q]][role] + combined[COMBINE[q]][role]:
+                    sent(kind, q)
 
 
 def shards_fused(tokens, chosen, gates, capacity, w_gate, w_up, w_down):
@@ -407,13 +475,16 @@
     chunks = width // LANES
     bf16, f32 = jnp.bfloat16, jnp.float32
     vmem = pl.BlockSpec(memory_space=pltpu.VMEM)
-    far = pl.BlockSpec(memory_space=pl.ANY)
+    far = pl.BlockSpec(memory_space=pltpu.HBM)
     return pl.pallas_call(
         fused,
-        out_shape=jax.ShapeDtypeStruct(tokens.shape, bf16),
-        in_specs=[pl.BlockSpec(memory_space=pltpu.SMEM), vmem, vmem, far, far, far, far],
+        out_shape=pltpu.VMEM(tokens.shape, bf16),
+        in_specs=[far] * 7,
         out_specs=vmem,
         scratch_shapes=[
+            pltpu.SMEM((1,), jnp.int32),
+            pltpu.VMEM((1, listed), jnp.int32),
+            pltpu.VMEM((1, listed), f32),
             pltpu.VMEM((block, width), bf16),
             pltpu.VMEM((chunks, 3 * block, LANES), bf16),
             pltpu.VMEM((listed, 4 * block), bf16),
@@ -441,13 +512,16 @@
             pltpu.VMEM((chunks, block, LANES), bf16),
             pltpu.VMEM((chunks, block, LANES), bf16),
             pltpu.VMEM((chunks, block, LANES), bf16),
-            pltpu.VMEM((2, chunks, block, LANES), bf16),
+            pltpu.VMEM((3, chunks, block, LANES), bf16),
             pltpu.VMEM((chunks, block, LANES), f32),
             pltpu.SemaphoreType.DMA((KINDS * chunks,)),
             pltpu.SemaphoreType.DMA((KINDS * chunks,)),
-            pltpu.SemaphoreType.DMA((12 + chunks,)),
+            pltpu.SemaphoreType.DMA((15 + chunks,)),
+            pltpu.SemaphoreType.DMA((4 * (chunks + 1),)),
+            pltpu.SemaphoreType.DMA((4 * (chunks + 1),)),
         ],
-        compiler_params=pltpu.CompilerParams(collective_id=0, has_side_effects=True),
+        compiler_params=pltpu.CompilerParams(
+            collective_id=0, has_side_effects=True, vmem_limit_bytes=VMEM_BYTES),
     )(capacity, chosen, gates, tokens, w_gate[0], w_up[0], w_down[0])
 
 

time: 55.5 us -> 53.2 us (0.959)
  Pallas kernels: 53 us -> 51.7 us
  local copies, waits for them, and re-layouts: 1.67 us -> 0.71 us
    pallas_call x1, Pallas kernels: 53 us -> 51.7 us  [shards_fused(): pl.pallas_call(fused, out_shape=pltpu.VMEM(tokens.shape, bf16), in_specs=...]
    unnamed x1, local copies, waits for them, and re-layouts: 1.67 us -> 0.71 us
where the time goes in v2:
time: 53.2 us; the launch traced here: 53 us
  Pallas kernels  51.7 us (97%)
  local copies, waits for them, and re-layouts  0.71 us (1%)
  between operations  0.66 us (1%)
    pallas_call x1, Pallas kernels, shards_fused(): pl.pallas_call(fused, out_shape=pltpu.VMEM(tokens.shape, bf16), in_specs=...  51.7 us

profile of v2, /device:TPU:0, one launch (start us, length us, event | category | flops | bytes accessed | tf_op | source)
XLA Modules:
  0.0 53.0 jit_solution(13851123661408210100)
XLA Ops:
  0.7 51.7 %shard_map.73 = bf16[256,512]{1,0:T(8,128)(2,1)S(1)} custom-call(s32[1]{0:T(128)S(6)} %copy.10.cap_hbm, s32[1,512]{1,0:T(1,128)} %chosen_hbm.1, f32[1,512]{1,0:T(1,128)} %gates_hbm.1, bf16[256,512]{1,0:T(8,128)(2,1)} %tok_hbm.1, bf16[2048,256]{1,0:T(8,128)(2,1)} %bitcast.3, bf16[2048,256]{1,0:T(8,128)(2,1)} %bitcast.4, bf16[256,2048]{1,0:T(8,128)(2,1)} %bitcast.5), custom_call_target="tpu_custom_call" | custom-call | tf_op jit(solution)/shard_map/pallas_call | solution.py:479
  52.3 0.7 %copy.9 = bf16[256,512]{1,0:T(8,128)(2,1)} copy(bf16[256,512]{1,0:T(8,128)(2,1)S(1)} %shard_map.73) | data formatting | bytes 524288

commit v3 on v2

--- a/solution.py
+++ b/solution.py
@@ -74,12 +74,20 @@
 LANES = 128
 MESH = pl.DeviceIdType.MESH
 KINDS = 20
-PIECES = 8
+PIECES = 2
 DISPATCH = ("plain", "plain", "plain", "merged")
 COMBINE = ("merged", "merged", "merged", "merged")
 VMEM_BYTES = 66 * 1000 * 1000
 (D_PAIR, D_PEER, D_CROSS, D_FAR, F_PEER, F_FAR, MERGED_A, MERGED_B, X_SAME, X_DIAG, X_MATE,
  Y_SAME, Y_DIAG, Y_MATE, C_FIRST, C_SECOND, P_PAIR, P_CROSS, P_PEER, IDS) = range(KINDS)
+
+BOTH = {X_SAME: 0, X_DIAG: 1, X_MATE: 2, Y_SAME: 3, Y_DIAG: 4, Y_MATE: 5}
+SENDS = 10
+SEND_AT = {**BOTH, D_PAIR: 6, D_PEER: 7, D_CROSS: 7, D_FAR: 9, F_PEER: 8, F_FAR: 9, MERGED_A: 8, MERGED_B: 9,
+           C_FIRST: 6, C_SECOND: 7, P_PAIR: 6, P_CROSS: 7, P_PEER: 8, IDS: 8}
+RECVS = 12
+RECV_AT = {**BOTH, D_PAIR: 6, D_PEER: 7, D_CROSS: 8, D_FAR: 8, F_PEER: 7, F_FAR: 8, MERGED_A: 7, MERGED_B: 8,
+           C_FIRST: 9, C_SECOND: 10, P_PAIR: 9, P_CROSS: 10, P_PEER: 11, IDS: RECVS}
 
 
 def dot(a, b):
@@ -95,7 +103,7 @@
     listed = chosen_ref.shape[1]
     half = listed // 2
     chunks = width // LANES
-    ff = wg_ref.shape[1]
+    ff = wg_ref.shape[2]
     bf16, f32 = jnp.bfloat16, jnp.float32
     z = lax.axis_index("expert")
     f = lax.axis_index("ffn")
@@ -120,23 +128,19 @@
     def cols(q):
         return slice(q * LANES, (q + 1) * LANES)
 
-    tok_loads = [pltpu.make_async_copy(tok_hbm.at[:, cols(q)], tok.at[:, cols(q)], load_sem.at[12 + q])
+    tok_loads = [pltpu.make_async_copy(tok_hbm.at[:, cols(q)], tok.at[:, cols(q)], load_sem.at[q])
                  for q in range(chunks)]
-    small_loads = [pltpu.make_async_copy(src, dst, load_sem.at[12 + chunks + i]) for i, (src, dst) in enumerate(
+    small_loads = [pltpu.make_async_copy(src, dst, load_sem.at[chunks + i]) for i, (src, dst) in enumerate(
         ((chosen_hbm, chosen_ref), (gates_hbm, gates_ref), (cap_hbm, cap_ref)))]
     for load in small_loads[:1] + tok_loads + small_loads[1:]:
         load.start()
-    loads = []
+    w_loads = [pltpu.make_async_copy(wg_ref, w_in.at[:, :, 0:ff], load_sem.at[chunks + 3]),
+               pltpu.make_async_copy(wu_ref, w_in.at[:, :, ff:2 * ff], load_sem.at[chunks + 4])]
     for s in range(4):
-        at = pl.ds(pl.multiple_of(slot_id[s] * width, width), width)
-        loads.append([
-            pltpu.make_async_copy(wg_ref.at[at, :], w_in.at[s, :, 0:ff], load_sem.at[3 * s]),
-            pltpu.make_async_copy(wu_ref.at[at, :], w_in.at[s, :, ff:2 * ff], load_sem.at[3 * s + 1]),
-            pltpu.make_async_copy(wd_ref.at[:, at], w_out.at[s], load_sem.at[3 * s + 2]),
-        ])
-    for group in loads:
-        for load in group:
-            load.start()
+        w_loads.append(pltpu.make_async_copy(
+            wd_ref.at[:, s * width:(s + 1) * width], w_out.at[s], load_sem.at[chunks + 5 + s]))
+    for load in w_loads:
+        load.start()
 
     def copy(kind, q):
         first, second = slice(0, half), slice(half, listed)
@@ -162,38 +166,25 @@
             P_PEER: lambda: (part_peer.at[q], part_in.at[2, q], to_mirror),
             IDS: lambda: (chosen_ref, ids_pair, to_pair),
         }[kind]()
-        i = kind * chunks + q
         return pltpu.make_async_remote_copy(
-            src_ref=src, dst_ref=dst, send_sem=send_sem.at[i], recv_sem=recv_sem.at[i],
-            device_id=to, device_id_type=MESH)
-
-    def w_copy(s, q):
+            src_ref=src, dst_ref=dst, send_sem=send_sem.at[SEND_AT[kind] * chunks + q],
+            recv_sem=recv_sem.at[RECV_AT[kind] * chunks + q], device_id=to, device_id_type=MESH)
+
+    def w_copy(q):
         if q < chunks:
-            src, dst = w_in.at[s, cols(q)], w_in_mate.at[s ^ 1, cols(q)]
+            src, dst = w_in.at[:, cols(q)], w_in_mate.at[:, cols(q)]
         else:
-            src, dst = w_out.at[s], w_out_mate.at[s ^ 1]
+            src, dst = w_out, w_out_mate
         return pltpu.make_async_remote_copy(
-            src_ref=src, dst_ref=dst, send_sem=w_send_sem.at[s * (chunks + 1) + q],
-            recv_sem=w_recv_sem.at[(s ^ 1) * (chunks + 1) + q], device_id=mate, device_id_type=MESH)
-
-    pieces = []
-    for q in range(chunks):
-        pieces += [(0, q), (1, q)]
-        if q >= 1:
-            pieces += [(2, q - 1), (3, q - 1)]
-    pieces += [(2, chunks - 1), (3, chunks - 1)] + [(s, chunks) for s in (2, 3, 0, 1)]
+            src_ref=src, dst_ref=dst, send_sem=w_send_sem.at[q], recv_sem=w_recv_sem.at[q],
+            device_id=mate, device_id_type=MESH)
 
     def push(left, number):
-        for s, q in left[:number]:
-            w_copy(s, q).start()
+        for q in left[:number]:
+            w_copy(q).start()
         return left[number:]
 
-    def push_some(left):
-        return push(left, 4)
-
-    def w_got(slots, q):
-        for s in slots:
-            w_copy(s ^ 1, q).wait_recv()
+    pieces = list(range(chunks + 1))
 
     def start(kind, q):
         copy(kind, q).start()
@@ -225,9 +216,8 @@
                 start(D_PAIR, q)
         small_loads[0].wait()
 
-    for group in loads:
-        for load in group:
-            load.wait()
+    for load in w_loads:
+        load.wait()
     for load in small_loads[1:]:
         load.wait()
     pieces = push(pieces, PIECES)
@@ -277,7 +267,7 @@
         at = slice(q * LANES, (q + 1) * LANES)
         lhs = jnp.concatenate(pieces, axis=1)
         for i, w in enumerate((w_in, w_in_mate)):
-            rhs = jnp.concatenate([w[s, at] for s in slots], axis=0)
+            rhs = jnp.concatenate([w[slot_id[s], at] for s in slots], axis=0)
             out = slice(i * 2 * ff, (i + 1) * 2 * ff)
             if begin:
                 acc[:, out] = dot(lhs, rhs)
@@ -286,13 +276,12 @@
 
     def add_chip(q):
         got(X_MATE, q)
-        w_got((0, 1), q)
+        w_copy(q).wait_recv()
         add(q, [rows[q, 0:half], x_mate[q]], (0, 1), q == 0)
 
     def add_across(q):
         got(X_SAME, q)
         got(X_DIAG, q)
-        w_got((2, 3), q)
         add(q, [x_in[0, q], x_in[1, q]], (2, 3))
 
     def behind(q):
@@ -322,7 +311,7 @@
                     start(kind, q)
             got(D_PAIR, q)
             send_rows(q, lambda: picked(pick, q, 0, True), lambda: picked(pick, q, 1, True))
-            left = push_some(left)
+            left = push(left, 1)
             behind(q)
 
     @pl.when(inner == 0)
@@ -348,7 +337,7 @@
                     return own + merged_in[q, at].astype(f32)
 
                 send_rows(q, lambda: from_pair(0, MERGED_A), lambda: from_pair(1, MERGED_B))
-            left = push_some(left)
+            left = push(left, 1)
             behind(q)
 
     add_chip(chunks - 1)
@@ -363,18 +352,20 @@
     def down(q, slots):
         total = None
         for i, w in enumerate((w_out, w_out_mate)):
-            part = dot(hid[i], jnp.concatenate([w[s, :, cols(q)] for s in slots], axis=1))
+            part = dot(hid[i], jnp.concatenate([w[slot_id[s], :, cols(q)] for s in slots], axis=1))
             total = part if total is None else total + part
         return total[:, :LANES], total[:, LANES:]
 
-    w_got((2, 3), chunks)
+    w_copy(chunks).wait_recv()
     for q in range(chunks):
         first, second = down(q, (2, 3))
         y_out[0, q] = first.astype(bf16)
-        start(Y_SAME, q)
         y_out[1, q] = second.astype(bf16)
-        start(Y_DIAG, q)
-    w_got((0, 1), chunks)
+        for value, kinds in ((0, (Y_SAME, Y_DIAG)), (1, (Y_DIAG, Y_SAME))):
+            @pl.when(core == value)
+            def _():
+                for kind in kinds:
+                    start(kind, q)
     for q in range(chunks):
         first, second = down(q, (0, 1))
         own_sum[q] = first
@@ -390,6 +381,34 @@
         got(Y_DIAG, q)
         other = y_in[2, q].astype(f32) + y_in[1, q].astype(f32)
         con[q, half:listed] = (live[half:listed] * other).astype(bf16)
+
+    combined = {"merged": ((C_FIRST, C_SECOND), (P_PAIR, P_CROSS, P_PEER)),
+                "direct": ((P_PAIR, P_CROSS, P_PEER),) * 2}
+    dispatched = {"plain": ((D_CROSS, D_PAIR), (D_PEER, D_PAIR, F_PEER, F_FAR)),
+                  "merged": ((D_CROSS, D_PAIR), (D_PEER, MERGED_A, MERGED_B)),
+                  "direct": ((D_CROSS, D_PAIR, D_FAR), (D_PEER, D_PAIR, F_PEER))}
+
+    def sent(kind, q):
+        copy(kind, q).wait_send()
+
+    def sent_first(role):
+        if role == 0:
+            sent(IDS, 0)
+        for q in range(chunks):
+            for kind in dispatched[DISPATCH[q]][role]:
+                sent(kind, q)
+
+    def sent_early():
+        for q in range(chunks):
+            for kind in BOTH:
+                sent(kind, q)
+        for q in range(chunks + 1):
+            w_copy(q).wait_send()
+
+    def sent_late(role):
+        for q in range(chunks):
+            for kind in combined[COMBINE[q]][role]:
+                sent(kind, q)
 
     def spread(q, order):
         for kind, part, slot in order:
@@ -407,6 +426,7 @@
 
     @pl.when(inner == 0)
     def _():
+        sent_first(0)
         for q in range(chunks):
             weigh_first(q)
             if COMBINE[q] == "merged":
@@ -417,11 +437,15 @@
             else:
                 spread(q, ((P_PEER, part_peer, 3), (P_CROSS, part_cross, 2), (P_PAIR, part_pair, 1)))
             own_out[q] = dot(put[0], con[q])
-        for q in range(chunks):
+        sent_early()
+        for q in range(chunks):
+            if q == chunks - 1:
+                sent_late(0)
             finish(q, every[:2] if COMBINE[q] == "merged" else every)
 
     @pl.when(inner == 1)
     def _():
+        sent_first(1)
         for q in range(chunks):
             weigh_first(q)
             weigh_second(q)
@@ -438,33 +462,11 @@
                     part[q] = (dot(put[mine], con[q]) + dot(put_pair[his], con_in[q])).astype(bf16)
                     start(kind, q)
                 own_out[q] = dot(put[0], con[q]) + dot(put_pair[0], con_in[q])
-        for q in range(chunks):
+        sent_early()
+        for q in range(chunks):
+            if q == chunks - 1:
+                sent_late(1)
             finish(q, every[2:] if COMBINE[q] == "merged" else every)
-
-    def sent(kind, q):
-        copy(kind, q).wait_send()
-
-    for q in range(chunks):
-        for kind in (X_SAME, X_DIAG, X_MATE, Y_SAME, Y_DIAG, Y_MATE):
-            sent(kind, q)
-    for s in range(4):
-        for q in range(chunks + 1):
-            w_copy(s, q).wait_send()
-
-    combined = {"merged": ((C_FIRST, C_SECOND), (P_PAIR, P_CROSS, P_PEER)),
-                "direct": ((P_PAIR, P_CROSS, P_PEER),) * 2}
-    dispatched = {"plain": ((D_CROSS, D_PAIR), (D_PEER, D_PAIR, F_PEER, F_FAR)),
-                  "merged": ((D_CROSS, D_PAIR), (D_PEER, MERGED_A, MERGED_B)),
-                  "direct": ((D_CROSS, D_PAIR, D_FAR), (D_PEER, D_PAIR, F_PEER))}
-
-    for role in range(2):
-        @pl.when(inner == role)
-        def _():
-            if role == 0:
-                sent(IDS, 0)
-            for q in range(chunks):
-                for kind in dispatched[DISPATCH[q]][role] + combined[COMBINE[q]][role]:
-                    sent(kind, q)
 
 
 def shards_fused(tokens, chosen, gates, capacity, w_gate, w_up, w_down):
@@ -514,15 +516,15 @@
             pltpu.VMEM((chunks, block, LANES), bf16),
             pltpu.VMEM((3, chunks, block, LANES), bf16),
             pltpu.VMEM((chunks, block, LANES), f32),
-            pltpu.SemaphoreType.DMA((KINDS * chunks,)),
-            pltpu.SemaphoreType.DMA((KINDS * chunks,)),
-            pltpu.SemaphoreType.DMA((15 + chunks,)),
-            pltpu.SemaphoreType.DMA((4 * (chunks + 1),)),
-            pltpu.SemaphoreType.DMA((4 * (chunks + 1),)),
+            pltpu.SemaphoreType.DMA((SENDS * chunks,)),
+            pltpu.SemaphoreType.DMA((RECVS * chunks + 1,)),
+            pltpu.SemaphoreType.DMA((chunks + 9,)),
+            pltpu.SemaphoreType.DMA((chunks + 1,)),
+            pltpu.SemaphoreType.DMA((chunks + 1,)),
         ],
         compiler_params=pltpu.CompilerParams(
             collective_id=0, has_side_effects=True, vmem_limit_bytes=VMEM_BYTES),
-    )(capacity, chosen, gates, tokens, w_gate[0], w_up[0], w_down[0])
+    )(capacity, chosen, gates, tokens, w_gate.reshape(-1, width, ff), w_up.reshape(-1, width, ff), w_down[0])
 
 
 def solution(mesh):

time: 53.2 us -> 51.6 us (0.970)
  Pallas kernels: 51.7 us -> 50.1 us
    pallas_call x1, Pallas kernels: 51.7 us -> 50.1 us  [shards_fused(): pl.pallas_call(fused, out_shape=pltpu.VMEM(tokens.shape, bf16), in_specs=...]
where the time goes in v3:
time: 51.6 us; the launch traced here: 51.5 us
  Pallas kernels  50.1 us (97%)
  local copies, waits for them, and re-layouts  0.71 us (1%)
  between operations  0.66 us (1%)
    pallas_call x1, Pallas kernels, shards_fused(): pl.pallas_call(fused, out_shape=pltpu.VMEM(tokens.shape, bf16), in_specs=...  50.1 us

profile of v3, /device:TPU:0, one launch (start us, length us, event | category | flops | bytes accessed | tf_op | source)
XLA Modules:
  0.0 51.5 jit_solution(2594638455122472402)
XLA Ops:
  0.7 50.1 %shard_map.73 = bf16[256,512]{1,0:T(8,128)(2,1)S(1)} custom-call(s32[1]{0:T(128)S(6)} %copy.10.cap_hbm, s32[1,512]{1,0:T(1,128)} %chosen_hbm.1, f32[1,512]{1,0:T(1,128)} %gates_hbm.1, bf16[256,512]{1,0:T(8,128)(2,1)} %tok_hbm.1, bf16[4,512,256]{2,1,0:T(8,128)(2,1)} %bitcast.3, bf16[4,512,256]{2,1,0:T(8,128)(2,1)} %bitcast.4, bf16[256,2048]{1,0:T(8,128)(2,1)} %bitcast.5), custom_call_target="tpu_custom_call" | custom-call | tf_op jit(solution)/shard_map/pallas_call | solution.py:481
  50.8 0.7 %copy.9 = bf16[256,512]{1,0:T(8,128)(2,1)} copy(bf16[256,512]{1,0:T(8,128)(2,1)S(1)} %shard_map.73) | data formatting | bytes 524288

commit v4 on v3

--- a/solution.py
+++ b/solution.py
@@ -204,8 +204,8 @@
         for q in range(chunks):
             tok_loads[q].wait()
             if mode(q) != "direct":
+                start(D_PAIR, q)
                 start(D_CROSS, q)
-                start(D_PAIR, q)
 
     @pl.when(inner == 1)
     def _():

time: 51.6 us -> 51.4 us (level)
  no operation moved by 1% of the time
where the time goes in v4:
time: 51.4 us; the launch traced here: 51.3 us
  Pallas kernels  49.9 us (97%)
  local copies, waits for them, and re-layouts  0.71 us (1%)
  between operations  0.66 us (1%)
    pallas_call x1, Pallas kernels, shards_fused(): pl.pallas_call(fused, out_shape=pltpu.VMEM(tokens.shape, bf16), in_specs=...  49.9 us

profile of v4, /device:TPU:0, one launch (start us, length us, event | category | flops | bytes accessed | tf_op | source)
XLA Modules:
  0.0 51.3 jit_solution(15535620815553441834)
XLA Ops:
  0.7 49.9 %shard_map.73 = bf16[256,512]{1,0:T(8,128)(2,1)S(1)} custom-call(s32[1]{0:T(128)S(6)} %copy.10.cap_hbm, s32[1,512]{1,0:T(1,128)} %chosen_hbm.1, f32[1,512]{1,0:T(1,128)} %gates_hbm.1, bf16[256,512]{1,0:T(8,128)(2,1)} %tok_hbm.1, bf16[4,512,256]{2,1,0:T(8,128)(2,1)} %bitcast.3, bf16[4,512,256]{2,1,0:T(8,128)(2,1)} %bitcast.4, bf16[256,2048]{1,0:T(8,128)(2,1)} %bitcast.5), custom_call_target="tpu_custom_call" | custom-call | tf_op jit(solution)/shard_map/pallas_call | solution.py:481
  50.6 0.7 %copy.9 = bf16[256,512]{1,0:T(8,128)(2,1)} copy(bf16[256,512]{1,0:T(8,128)(2,1)S(1)} %shard_map.73) | data formatting | bytes 524288
